TPU v7x, 32 devices: a whole 2x2x4 slice. The times are simulated.
32 devices in a mesh: dp: 16 (over z, y, x), mp: 2 (over core).
Axes of the slice: x: 2, y: 2, z: 4, core: 2. Of those that a mesh axis runs over, the one named last changes fastest.
Arguments:
- pooled_grad: bfloat16 [4096, 32, 128], P(('dp', 'mp')), may hold values from -6 to 6
- bag_lengths: int32 [4096, 32], P(('dp', 'mp')), may hold values from 1 to 4
- bag_rows: int32 [4096, 32, 4], P(('dp', 'mp')), may hold values from 0 to 2047
- table_rows: float32 [32, 2048, 128], P('dp', 'mp'), may hold values from -6 to 6
- row_accum: float32 [32, 2048], P('dp', 'mp'), may hold values from 0.01 to 1
- dense_input: bfloat16 [4096, 1024], P(('dp', 'mp')), may hold values from -6 to 6
- dense_cotangent: bfloat16 [4096, 1024], P(('dp', 'mp')), may hold values from -0.09375 to 0.09375
Outputs:
- new_rows: float32 [32, 2048, 128], P('dp', 'mp')
- new_accum: float32 [32, 2048], P('dp', 'mp')
- dense_grad: float32 [1024, 1024], replicated
Inputs may be any that keep to these rules, and one draw needn't show every extreme that they name: `bag_rows`: a row number of the whole table.
All inputs are finite; a program needn't handle non-finite values.
Results may differ from a plain program's by a relative error of at most 0.0003.
Values may be sent and summed in bfloat16 or wider, within the bound.
A program may use at most 128 MiB of HBM per device.

v0:
```python
import math

import jax
import jax.numpy as jnp
from jax import lax
from jax.sharding import PartitionSpec as P

learn_rate = 0.5


def grads_by_row(grads, lengths, looked, base_row, row_count):
    sample_count = grads.shape[0]
    tab_local = grads.shape[1]
    feat_width = grads.shape[2]
    slot_count = looked.shape[2]
    step = math.gcd(sample_count, max(8, (1 << 21) // row_count))
    turns = sample_count // step
    slot_iota = jnp.arange(slot_count, dtype=jnp.int32)
    target = jnp.where(slot_iota[None, None, :] < lengths[..., None], looked - base_row, -1)
    row_iota = jnp.arange(row_count, dtype=jnp.int32)
    results = []
    for table in range(tab_local):

        def add_block(turn, total):
            start = turn * step
            piece = lax.dynamic_slice_in_dim(grads, start, step, 0)[:, table, :]
            wanted = lax.dynamic_slice_in_dim(target, start, step, 0)[:, table, :]
            onehot = (wanted[:, 0, None] == row_iota[None, :]).astype(jnp.bfloat16)
            for slot in range(1, slot_count):
                onehot = onehot + (wanted[:, slot, None] == row_iota[None, :]).astype(jnp.bfloat16)
            return total + lax.dot_general(
                onehot, piece, (((0,), (0,)), ((), ())), preferred_element_type=jnp.float32
            )

        empty = jnp.zeros((row_count, feat_width), jnp.float32)
        results.append(lax.fori_loop(0, turns, add_block, empty))
    return jnp.stack(results, axis=0)


def per_device(
    pooled_grad, bag_lengths, bag_rows, table_rows, row_accum, dense_input, dense_cotangent
):
    local_dense = lax.dot_general(
        dense_input, dense_cotangent, (((0,), (0,)), ((), ())), preferred_element_type=jnp.float32
    )
    dense_grad = lax.psum(local_dense, ("dp", "mp"))
    rows_local = table_rows.shape[1]
    base_row = lax.axis_index("mp") * rows_local
    owned_grad, owned_lengths, owned_rows = (
        lax.all_to_all(pooled_grad, "dp", split_axis=1, concat_axis=0, tiled=True),
        lax.all_to_all(bag_lengths, "dp", split_axis=1, concat_axis=0, tiled=True),
        lax.all_to_all(bag_rows, "dp", split_axis=1, concat_axis=0, tiled=True),
    )
    gathered, lengths_all, rows_all = (
        lax.all_gather(owned_grad, "mp", axis=0, tiled=True),
        lax.all_gather(owned_lengths, "mp", axis=0, tiled=True),
        lax.all_gather(owned_rows, "mp", axis=0, tiled=True),
    )
    row_grad = grads_by_row(gathered, lengths_all, rows_all, base_row, rows_local)
    new_accum = row_accum + jnp.mean(row_grad * row_grad, axis=-1)
    new_rows = table_rows - learn_rate * row_grad / jnp.sqrt(new_accum)[..., None]
    return (new_rows, new_accum, dense_grad)


def solution(mesh):
    in_specs = (
        P(("dp", "mp"), None, None),
        P(("dp", "mp"), None),
        P(("dp", "mp"), None, None),
        P("dp", "mp", None),
        P("dp", "mp"),
        P(("dp", "mp"), None),
        P(("dp", "mp"), None),
    )
    out_specs = (P("dp", "mp", None), P("dp", "mp"), P())
    return jax.shard_map(
        per_device, mesh=mesh, in_specs=in_specs, out_specs=out_specs, check_vma=False
    )
```

profile of v0, /device:TPU:11, one launch (start us, length us, event | category | flops | bytes accessed | tf_op | source)
XLA Modules:
  0.0 218.3 jit_solution(12883736953715201014)
XLA Ops:
  8.0 0.0 copy-start
  8.0 0.0 copy-start.3
  8.0 0.0 copy-start.2
  8.0 0.0 all-gather.2.cloned.1.call-start
  8.1 1.7 copy.18
  9.8 30.4 %all_to_all.55 = bf16[128,32,128]{2,0,1:T(8,128)(2,1)S(1)} all-to-all(bf16[128,32,128]{2,0,1:T(8,128)(2,1)S(1)} %copy.18), channel_id=1, replica_groups=mesh['dp'=16,'mp'=2] {'dp'}, dimensions={1} | all-to-all | bytes 2097152 | tf_op jit(solution)/shard_map/all_to_all | solution.py:50
  40.2 1.0 copy.19
  41.2 0.0 all-gather.2.cloned.1.call-update
  41.3 0.0 copy-done.3
  41.3 9.6 %all_to_all.56 = s32[128,16,2]{0,2,1:T(2,128)S(1)} all-to-all(s32[128,16,2]{0,2,1:T(2,128)S(1)} %bitcast.79), channel_id=1, replica_groups=mesh['dp'=16,'mp'=2] {'dp'}, dimensions={1} | all-to-all | bytes 32768 | tf_op jit(solution)/shard_map/all_to_all | solution.py:51
  50.8 5.4 %all-to-all-start.1 = ((s32[128,32,4]{0,2,1:T(4,128)}), s32[128,32,4]{0,2,1:T(4,128)S(1)}, u32[]{:S(2)}, u32[]{:S(2)}) async-start(s32[128,32,4]{0,2,1:T(4,128)} %param.13), calls=%async_computation.1 | async-start | bytes 131072 | tf_op jit(solution)/shard_map/all_to_all | solution.py:52
  56.2 0.0 all-reduce.2.cloned.1.call-start
  56.3 0.0 copy-done
  56.3 0.0 copy-done.2
  56.3 2.7 %fusion.47 = f32[1024,1024]{1,0:T(8,128)} fusion(bf16[128,1024]{1,0:T(8,128)(2,1)S(1)} %copy-done, bf16[128,1024]{1,0:T(8,128)(2,1)S(1)} %copy-done.2), kind=kOutput, calls=%fused_computation.52 | convolution fusion | flops 268435456 | bytes 4718592 | tf_op jit(solution)/shard_map/dot_general | solution.py:43
  59.0 0.0 all-reduce.2.cloned.1.call-update
  59.1 4.6 %all_gather.9 = s32[4096,2]{0,1:T(2,128)S(1)} all-gather(s32[2048,2]{0,1:T(2,128)S(1)} %bitcast.78), channel_id=1, replica_groups=mesh['dp'=16,'mp'=2] {'mp'}, dimensions={0}, use_global_device_ids=true | all-gather | bytes 49152 | tf_op jit(solution)/shard_map/all_gather | solution.py:56
  63.7 0.0 all-to-all-done.1
  63.7 2.6 %all_gather.10 = s32[4096,2,4]{0,2,1:T(4,128)S(1)} all-gather(s32[2048,2,4]{0,2,1:T(4,128)S(1)} %all_to_all.47), channel_id=1, replica_groups=mesh['dp'=16,'mp'=2] {'mp'}, dimensions={0}, use_global_device_ids=true | all-gather | bytes 196608 | tf_op jit(solution)/shard_map/all_gather | solution.py:57
  66.4 0.0 all-gather.2.cloned.1.call-done
  66.4 11.6 %while.31 = (s32[]{:T(128)}, f32[1024,128]{1,0:T(8,128)S(1)}, s32[4096,2,4]{0,2,1:T(4,128)S(1)}, bf16[4096,2,128]{2,0,1:T(8,128)(2,1)}, s32[]{:T(128)}, /*index=5*/s32[]{:T(128)}, s32[]{:T(128)}, s32[]{:T(128)}, s32[]{}) while((s32[]{:T(128)}, f32[1024,128]{1,0:T(8,128)S(1)}, s32[4096,2,4]{0,2,1:T(4,128)S(1)}, ...), condition=%wide.region_3.4_spmd.clone.clone, body=%wide.region_2.3_spmd.clone.clone.sunk | while | flops 570687488 | bytes 1736889 | solution.py:36
  66.5 5.7 %fusion.61 = f32[1024,128]{1,0:T(8,128)S(1)} fusion(s32[2048]{0:T(1024)S(1)} %bitcast.71, s32[2048]{0:T(1024)S(1)} %bitcast.72, s32[2048]{0:T(1024)S(1)} %bitcast.73, s32[2048]{0:T(1024)S(1)} %bitcast.70, bf16[4096,2,128]{2,0,1:T(8,128)(2,1)} %get-tuple-element.390, s32[]{:T(128)S(6)} %select_n.29, s32[]{:T(128)S(6)} %add.197, ...), kind=kOutput, calls=%fused_computation.38.clone.1 | convolution fusion | flops 570687488 | bytes 1605641 | tf_op jit(solution)/shard_map/while/body/eval_jaxpr/dot_general | solution.py:31
  72.3 5.8 %fusion.61 = f32[1024,128]{1,0:T(8,128)S(1)} fusion(s32[2048]{0:T(1024)S(1)} %bitcast.71, s32[2048]{0:T(1024)S(1)} %bitcast.72, s32[2048]{0:T(1024)S(1)} %bitcast.73, s32[2048]{0:T(1024)S(1)} %bitcast.70, bf16[4096,2,128]{2,0,1:T(8,128)(2,1)} %get-tuple-element.390, s32[]{:T(128)S(6)} %select_n.29, s32[]{:T(128)S(6)} %add.197, ...), kind=kOutput, calls=%fused_computation.38.clone.1 | convolution fusion | flops 570687488 | bytes 1605641 | tf_op jit(solution)/shard_map/while/body/eval_jaxpr/dot_general | solution.py:31
  78.0 0.0 copy-start.4
  78.1 0.0 copy-start.1
  78.1 11.7 %while.30 = (s32[]{:T(128)}, f32[1024,128]{1,0:T(8,128)S(1)}, s32[4096,2,4]{0,2,1:T(4,128)S(1)}, bf16[4096,2,128]{2,0,1:T(8,128)(2,1)}, s32[]{:T(128)}, /*index=5*/s32[]{:T(128)}, s32[]{:T(128)}, s32[]{:T(128)}) while((s32[]{:T(128)}, f32[1024,128]{1,0:T(8,128)S(1)}, s32[4096,2,4]{0,2,1:T(4,128)S(1)}, ...), condition=%wide.region_1.2_spmd.clone.clone, body=%wide.region_0.0_spmd.clone.clone.sunk | while | flops 570687488 | bytes 1736861 | solution.py:36
  78.1 5.8 %fusion.58 = f32[1024,128]{1,0:T(8,128)S(1)} fusion(s32[2048]{0:T(1024)S(1)} %bitcast.75, s32[2048]{0:T(1024)S(1)} %bitcast.76, s32[2048]{0:T(1024)S(1)} %bitcast.77, s32[2048]{0:T(1024)S(1)} %bitcast.74, bf16[4096,2,128]{2,0,1:T(8,128)(2,1)} %get-tuple-element.415, s32[]{:T(128)S(6)} %select_n.28, f32[1024,128]{1,0:T(8,128)S(1)} %get-tuple-element.405, ...), kind=kOutput, calls=%fused_computation.18.clone.1 | convolution fusion | flops 570687488 | bytes 1605637 | tf_op jit(solution)/shard_map/while/body/eval_jaxpr/dot_general | solution.py:31
  84.0 5.7 %fusion.58 = f32[1024,128]{1,0:T(8,128)S(1)} fusion(s32[2048]{0:T(1024)S(1)} %bitcast.75, s32[2048]{0:T(1024)S(1)} %bitcast.76, s32[2048]{0:T(1024)S(1)} %bitcast.77, s32[2048]{0:T(1024)S(1)} %bitcast.74, bf16[4096,2,128]{2,0,1:T(8,128)(2,1)} %get-tuple-element.415, s32[]{:T(128)S(6)} %select_n.28, f32[1024,128]{1,0:T(8,128)S(1)} %get-tuple-element.405, ...), kind=kOutput, calls=%fused_computation.18.clone.1 | convolution fusion | flops 570687488 | bytes 1605637 | tf_op jit(solution)/shard_map/while/body/eval_jaxpr/dot_general | solution.py:31
  89.8 0.4 multiply_reduce_fusion
  90.1 0.0 copy-done.4
  90.1 0.6 fusion.44
  90.7 0.0 copy-done.1
  90.7 1.3 divide_subtract_fusion
  92.0 114.0 %all-reduce.2.cloned.1.call-done = f32[1024,1024]{1,0:T(8,128)} async-done(((f32[1024,1024]{1,0:T(8,128)}), f32[1024,1024]{1,0:T(8,128)}) %all-reduce.2.cloned.1.call-update) | async-done | bytes 4194320 | tf_op jit(solution)/shard_map/psum | solution.py:46
  206.1 4.8 %copy.35 = f32[1024,1024]{1,0:T(8,128)} copy(f32[1024,1024]{1,0:T(8,128)} %all-reduce.2.cloned.1.call-done) | data formatting | bytes 8388608
  (13 shorter events, 0.2 us)
Async XLA Ops:
  8.0 48.3 %copy-start = (bf16[128,1024]{1,0:T(8,128)(2,1)S(1)}, bf16[128,1024]{1,0:T(8,128)(2,1)}, u32[]{:S(2)}) copy-start(bf16[128,1024]{1,0:T(8,128)(2,1)} %param.16) | copy-start | bytes 786436
  8.0 33.2 %copy-start.3 = (s32[128,32]{0,1:T(8,128)S(1)}, s32[128,32]{0,1:T(8,128)}, u32[]{:S(2)}) copy-start(s32[128,32]{0,1:T(8,128)} %param.12) | copy-start | bytes 49156
  8.0 48.2 %copy-start.2 = (bf16[128,1024]{1,0:T(8,128)(2,1)S(1)}, bf16[128,1024]{1,0:T(8,128)(2,1)}, u32[]{:S(2)}) copy-start(bf16[128,1024]{1,0:T(8,128)(2,1)} %param.17) | copy-start | bytes 786436
  8.0 58.4 %all-gather.2.cloned.1.call-start = ((), (), s32[]{:S(2)}) async-start(), calls=%async_computation.3 | async-start | bytes 3145728 | tf_op jit(solution)/shard_map/all_gather | solution.py:55
  50.8 12.8 %all-to-all-start.1 = ((s32[128,32,4]{0,2,1:T(4,128)}), s32[128,32,4]{0,2,1:T(4,128)S(1)}, u32[]{:S(2)}, u32[]{:S(2)}) async-start(s32[128,32,4]{0,2,1:T(4,128)} %param.13), calls=%async_computation.1 | async-start | bytes 131072 | tf_op jit(solution)/shard_map/all_to_all | solution.py:52
  56.2 149.8 %all-reduce.2.cloned.1.call-start = ((), (), s32[]{:S(2)}) async-start(), calls=%async_computation.4 | async-start | bytes 8388608 | tf_op jit(solution)/shard_map/psum | solution.py:46
  78.0 12.1 %copy-start.4 = (f32[2,1024]{1,0:T(2,128)S(1)}, f32[2,1024]{1,0:T(2,128)}, u32[]{:S(2)}) copy-start(f32[2,1024]{1,0:T(2,128)} %param.15) | copy-start | bytes 24580
  78.1 12.7 %copy-start.1 = (f32[2,1024,128]{2,1,0:T(8,128)S(1)}, f32[2,1024,128]{2,1,0:T(8,128)}, u32[]{:S(2)}) copy-start(f32[2,1024,128]{2,1,0:T(8,128)} %param.14) | copy-start | bytes 3145732
Sparse Core Ops, SparseCore 0:
  41.4 12.0 all-gather.1
Sparse Core Ops, SparseCore 1:
  62.8 143.2 all-reduce.1
where the time goes:
time: 222 us; the launch traced here: 218 us
  waiting for transfers between devices  114 us (51%)
  blocking collectives  47.2 us (21%)
  matrix products  25.7 us (12%)
  between operations  15.6 us (7%)
  local copies, waits for them, and re-layouts  7.72 us (3%)
  starting transfers between devices  5.46 us (2%)
  other arithmetic  2.32 us (1%)
    psum x1, waiting for transfers between devices, per_device(): dense_grad = lax.psum(local_dense, ('dp', 'mp'))  114 us
    all_to_all x1, blocking collectives, per_device(): lax.all_to_all(pooled_grad, 'dp', split_axis=1, concat_axis=0, tiled=True)  30.4 us
    dot_general x4, matrix products, add_block(): lax.dot_general(onehot, piece, (((0,), (0,)), ((), ())), preferred_elemen...  23 us
    all_to_all x1, blocking collectives, per_device(): lax.all_to_all(bag_lengths, 'dp', split_axis=1, concat_axis=0, tiled=True)  9.57 us
    unnamed x12, local copies, waits for them, and re-layouts  6.5 us
    all_to_all x1, starting transfers between devices, per_device(): lax.all_to_all(bag_rows, 'dp', split_axis=1, concat_axis=0, tiled=True)  5.38 us
    all_gather x1, blocking collectives, per_device(): lax.all_gather(owned_lengths, 'mp', axis=0, tiled=True)  4.59 us
  transfers between devices with their start and end apart: 3, of which 1 were waited for; matrix products, arithmetic and copies ran while one was open for 13% of the time, Pallas kernels for 0%

commit v1 on v0

v1 whole, which is shorter than its diff:
```python
import functools

import jax
import jax.numpy as jnp
from jax import lax
from jax.experimental import pallas as pl
from jax.experimental.pallas import tpu as pltpu
from jax.sharding import PartitionSpec as P

learn_rate = 0.5
MESH = pl.DeviceIdType.MESH


def loop(count, body):
    def step(k, carry):
        body(k)
        return carry

    lax.fori_loop(0, count, step, 0)


def exchange_kernel(
    dp, mp, inner, row_parts,
    g_ref, i_ref, din_ref, dcot_ref,
    gbuf, ibuf, dense,
    abuf, bbuf, part, rbuf,
    a_send, a_recv, b_send, b_recv, g_send, g_recv, i_send, i_recv,
    gf_send, gf_recv, if_send, if_recv,
    r_send, r_recv, z_send, z_recv, x_send, x_recv, m_send, m_recv,
):
    me = lax.axis_index("dp")
    m = lax.axis_index("mp")
    outer = dp // inner
    z, i = me // inner, me % inner
    group = inner * mp
    col_parts = group // row_parts
    rows, cols = dense.shape[0] // row_parts, dense.shape[1] // col_parts
    piece = rows // outer
    mine = i * mp + m

    barrier = pltpu.get_barrier_semaphore()

    def signal(d, q):
        pl.semaphore_signal(barrier, inc=1, device_id=(d, q), device_id_type=MESH)

    loop(dp - 1, lambda k: signal((me + 1 + k) % dp, m))
    loop((mp - 1) * inner, lambda k: signal(z * inner + k % inner, (m + 1 + k // inner) % mp))
    pl.semaphore_wait(barrier, dp - 1 + (mp - 1) * inner)

    def remote(src, dst, send, recv, d, q):
        return pltpu.make_async_remote_copy(
            src_ref=src, dst_ref=dst, send_sem=send, recv_sem=recv, device_id=(d, q), device_id_type=MESH
        )

    def row_span(p):
        return pl.ds(pl.multiple_of((p // col_parts) * rows, 128), rows)

    def col_span(p):
        return pl.ds(pl.multiple_of((p % col_parts) * cols, 128), cols)

    def a_copy(k):
        p = (mine + 1 + k) % group
        return remote(din_ref.at[:, row_span(p)], abuf.at[mine], a_send.at[k], a_recv.at[mine], z * inner + p // mp, p % mp)

    def b_copy(k):
        p = (mine + 1 + k) % group
        return remote(dcot_ref.at[:, col_span(p)], bbuf.at[mine], b_send.at[k], b_recv.at[mine], z * inner + p // mp, p % mp)

    def start_dense(k):
        a_copy(k).start()
        b_copy(k).start()

    loop(group - 1, start_dense)

    def g_copy(k):
        d = (me + 1 + k) % dp
        return remote(g_ref.at[d], gbuf.at[me, m], g_send.at[k], g_recv.at[me], d, m)

    def i_copy(k):
        d = (me + 1 + k) % dp
        return remote(i_ref.at[d], ibuf.at[me, m], i_send.at[k], i_recv.at[me], d, m)

    def start_grads(k):
        g_copy(k).start()
        i_copy(k).start()

    loop(dp - 1, start_grads)

    def forward(s, k, src_g, src_i):
        q = (m + 1 + k) % mp
        return (
            remote(src_g, gbuf.at[s, m], gf_send.at[k, s], gf_recv.at[m, s], me, q),
            remote(src_i, ibuf.at[s, m], if_send.at[k, s], if_recv.at[m, s], me, q),
        )

    def start_forward(s, src_g, src_i):
        for k in range(mp - 1):
            for copy in forward(s, k, src_g, src_i):
                copy.start()

    start_forward(me, g_ref.at[me], i_ref.at[me])
    gbuf[me, m] = g_ref[me]
    ibuf[me, m] = i_ref[me]
    abuf[mine] = din_ref[:, row_span(mine)]
    bbuf[mine] = dcot_ref[:, col_span(mine)]

    def wait_dense(k):
        s = (mine + 1 + k) % group
        remote(abuf.at[s], abuf.at[s], a_send.at[k], a_recv.at[s], me, m).wait_recv()
        remote(bbuf.at[s], bbuf.at[s], b_send.at[k], b_recv.at[s], me, m).wait_recv()

    loop(group - 1, wait_dense)
    depth = abuf.shape[0] * abuf.shape[1]
    part[...] = lax.dot_general(
        abuf[...].reshape(depth, rows), bbuf[...].reshape(depth, cols), (((0,), (0,)), ((), ())),
        preferred_element_type=jnp.float32,
    )

    def piece_of(ref, w):
        return ref.at[pl.ds(pl.multiple_of(w * piece, 8), piece)]

    def r_copy(k):
        w = (z + 1 + k) % outer
        return remote(piece_of(part, w), rbuf.at[z], r_send.at[k], r_recv.at[z], w * inner + i, m)

    loop(outer - 1, lambda k: r_copy(k).start())
    own = part[pl.ds(pl.multiple_of(z * piece, 8), piece)]

    def spot(j, q, w):
        p = j * mp + q
        top = pl.multiple_of((p // col_parts) * rows + w * piece, 8)
        return pl.ds(top, piece), col_span(p)

    def at(j, q, w):
        return dense.at[spot(j, q, w)]

    rbuf[z] = own

    def wait_sum(k):
        s = (z + 1 + k) % outer
        remote(rbuf.at[s], rbuf.at[s], r_send.at[k], r_recv.at[s], me, m).wait_recv()

    loop(outer - 1, wait_sum)
    total = rbuf[0]
    for w in range(1, outer):
        total = total + rbuf[w]
    dense[spot(i, m, z)] = total

    def z_copy(k):
        w = (z + 1 + k) % outer
        return remote(at(i, m, z), at(i, m, z), z_send.at[k], z_recv.at[z], w * inner + i, m)

    def x_copy(k, w):
        j = (i + 1 + k) % inner
        return remote(at(i, m, w), at(i, m, w), x_send.at[k, w], x_recv.at[i, w], z * inner + j, m)

    def m_copy(k, j, w):
        return remote(at(j, m, w), at(j, m, w), m_send.at[k, j, w], m_recv.at[m, j, w], me, (m + 1 + k) % mp)

    def spread(w):
        loop(inner - 1, lambda k: x_copy(k, w).start())
        for k in range(mp - 1):
            m_copy(k, i, w).start()

    loop(outer - 1, lambda k: z_copy(k).start())
    spread(z)

    def pass_grads(k):
        s = (me + dp - 1 - k) % dp
        remote(gbuf.at[s, m], gbuf.at[s, m], g_send.at[k], g_recv.at[s], me, m).wait_recv()
        remote(ibuf.at[s, m], ibuf.at[s, m], i_send.at[k], i_recv.at[s], me, m).wait_recv()
        start_forward(s, gbuf.at[s, m], ibuf.at[s, m])

    def pass_piece(k):
        w = (z + 1 + k) % outer
        remote(at(i, m, w), at(i, m, w), z_send.at[k], z_recv.at[w], me, m).wait_recv()
        spread(w)

    loop(dp - 1, pass_grads)
    loop(outer - 1, pass_piece)

    def pass_block(t):
        k, w = t % (inner - 1), (z + t // (inner - 1)) % outer
        j = (i + 1 + k) % inner
        remote(at(j, m, w), at(j, m, w), x_send.at[k, w], x_recv.at[j, w], me, m).wait_recv()
        for n in range(mp - 1):
            m_copy(n, j, w).start()

    loop((inner - 1) * outer, pass_block)

    def end_forward(s):
        for k in range(mp - 1):
            q = (m + 1 + k) % mp
            remote(gbuf.at[s, q], gbuf.at[s, q], gf_send.at[k, s], gf_recv.at[q, s], me, m).wait_recv()
            remote(ibuf.at[s, q], ibuf.at[s, q], if_send.at[k, s], if_recv.at[q, s], me, m).wait_recv()
            for copy in forward(s, k, gbuf.at[s, m], ibuf.at[s, m]):
                copy.wait_send()

    loop(dp, end_forward)

    def end_block(t):
        j, w = t // outer, t % outer
        for k in range(mp - 1):
            q = (m + 1 + k) % mp
            remote(at(j, q, w), at(j, q, w), m_send.at[k, j, w], m_recv.at[q, j, w], me, m).wait_recv()
            m_copy(k, j, w).wait_send()

    loop(inner * outer, end_block)

    def end_dense(k):
        a_copy(k).wait_send()
        b_copy(k).wait_send()

    def end_grads(k):
        g_copy(k).wait_send()
        i_copy(k).wait_send()

    loop(group - 1, end_dense)
    loop(dp - 1, end_grads)

    def end_sum(k):
        r_copy(k).wait_send()
        z_copy(k).wait_send()

    loop(outer - 1, end_sum)
    loop((inner - 1) * outer, lambda t: x_copy(t % (inner - 1), t // (inner - 1)).wait_send())


def rows_kernel(slots, chunk, g_ref, i_ref, out_ref):
    tables, row_count = out_ref.shape[0], out_ref.shape[1]
    samples = i_ref.shape[2]
    base = lax.axis_index("mp") * row_count
    row_iota = lax.broadcasted_iota(jnp.int32, (row_count, samples), 0) + base
    out_ref[...] = jnp.zeros_like(out_ref)

    def add(c):
        for t in range(tables):
            hots = []
            for u in range(chunk):
                wanted = i_ref[c * chunk + u]
                hot = jnp.zeros((row_count, samples), jnp.float32)
                for s in range(slots):
                    one = wanted[t * slots + s : t * slots + s + 1, :]
                    hot = hot + jnp.where(row_iota == one, 1.0, 0.0)
                hots.append(hot.astype(jnp.bfloat16))
            onehot = jnp.concatenate(hots, axis=1)
            values = g_ref[pl.ds(c * chunk, chunk), t].reshape(chunk * samples, g_ref.shape[3])
            out_ref[t] += jnp.dot(onehot, values, preferred_element_type=jnp.float32)

    loop(i_ref.shape[0] // chunk, add)


def per_device(dp, mp, pooled_grad, bag_lengths, bag_rows, table_rows, row_accum, dense_input, dense_cotangent):
    samples, all_tables, width = pooled_grad.shape
    slots = bag_rows.shape[2]
    tables, row_count = table_rows.shape[0], table_rows.shape[1]
    inner = 4 if dp % 4 == 0 else 1
    outer = dp // inner
    group = inner * mp
    row_parts = 2 if group % 2 == 0 else 1
    in_width, out_width = dense_input.shape[1], dense_cotangent.shape[1]
    rows, cols = in_width // row_parts, out_width // (group // row_parts)

    slot_iota = jnp.arange(slots, dtype=jnp.int32)
    target = jnp.where(slot_iota[None, None, :] < bag_lengths[..., None], bag_rows, -1)
    target = target.transpose(1, 2, 0).reshape(dp, tables * slots, samples)
    grads = pooled_grad.transpose(1, 0, 2).reshape(dp, tables, samples, width)

    vmem = pl.BlockSpec(memory_space=pltpu.VMEM)
    dma = pltpu.SemaphoreType.DMA
    pairs = max(1, mp - 1)
    gathered, targets, dense_grad = pl.pallas_call(
        functools.partial(exchange_kernel, dp, mp, inner, row_parts),
        out_shape=(
            jax.ShapeDtypeStruct((dp, mp, tables, samples, width), jnp.bfloat16),
            jax.ShapeDtypeStruct((dp, mp, tables * slots, samples), jnp.int32),
            jax.ShapeDtypeStruct((in_width, out_width), jnp.float32),
        ),
        in_specs=[vmem] * 4,
        out_specs=(vmem,) * 3,
        scratch_shapes=[
            pltpu.VMEM((group, samples, rows), jnp.bfloat16),
            pltpu.VMEM((group, samples, cols), jnp.bfloat16),
            pltpu.VMEM((rows, cols), jnp.float32),
            pltpu.VMEM((outer, rows // outer, cols), jnp.float32),
            dma((group,)), dma((group,)), dma((group,)), dma((group,)),
            dma((dp,)), dma((dp,)), dma((dp,)), dma((dp,)),
            dma((pairs, dp)), dma((mp, dp)), dma((pairs, dp)), dma((mp, dp)),
            dma((outer,)), dma((outer,)), dma((outer,)), dma((outer,)),
            dma((inner, outer)), dma((inner, outer)),
            dma((pairs, inner, outer)), dma((mp, inner, outer)),
        ],
        compiler_params=pltpu.CompilerParams(collective_id=0, has_side_effects=True),
        name="exchange",
    )(grads, target, dense_input, dense_cotangent)

    sources = dp * mp
    row_grad = pl.pallas_call(
        functools.partial(rows_kernel, slots, 2 if sources % 2 == 0 else 1),
        out_shape=jax.ShapeDtypeStruct((tables, row_count, width), jnp.float32),
        in_specs=[vmem] * 2,
        out_specs=vmem,
        name="rows",
    )(gathered.reshape(sources, tables, samples, width), targets.reshape(sources, tables * slots, samples))

    new_accum = row_accum + jnp.mean(row_grad * row_grad, axis=-1)
    new_rows = table_rows - learn_rate * row_grad / jnp.sqrt(new_accum)[..., None]
    return (new_rows, new_accum, dense_grad)


def solution(mesh):
    in_specs = (
        P(("dp", "mp"), None, None),
        P(("dp", "mp"), None),
        P(("dp", "mp"), None, None),
        P("dp", "mp", None),
        P("dp", "mp"),
        P(("dp", "mp"), None),
        P(("dp", "mp"), None),
    )
    out_specs = (P("dp", "mp", None), P("dp", "mp"), P())
    body = functools.partial(per_device, mesh.shape["dp"], mesh.shape["mp"])
    return jax.shard_map(body, mesh=mesh, in_specs=in_specs, out_specs=out_specs, check_vma=False)
```

time: 222 us -> 109 us (0.49); the launches traced: 218 us -> 109 us
  waiting for transfers between devices: 114 us -> 0 us
  Pallas kernels: 0 us -> 97.1 us
  blocking collectives: 47.2 us -> 0 us
  matrix products: 25.7 us -> 0 us
  between operations: 15.6 us -> 0.67 us
  starting transfers between devices: 5.46 us -> 0 us
  other arithmetic: 2.32 us -> 6.45 us
  local copies, waits for them, and re-layouts: 7.72 us -> 4.63 us
    psum x1 -> x0, waiting for transfers between devices: 114 us -> none  [per_device(): dense_grad = lax.psum(local_dense, ('dp', 'mp'))]
    pallas_call x0 -> x2, Pallas kernels: none -> 97.1 us  [the longest x1 79.5 us: per_device(): pl.pallas_call(functools.partial(exchange_kernel, dp, mp, inner, row_part...]
    all_to_all x2 -> x0, blocking collectives: 40 us -> none  [the longest x1 30.4 us: per_device(): lax.all_to_all(pooled_grad, 'dp', split_axis=1, concat_axis=0, tiled=True)]
    dot_general x5 -> x0, matrix products: 25.7 us -> none  [the longest x4 23 us: add_block(): lax.dot_general(onehot, piece, (((0,), (0,)), ((), ())), preferred_elemen...]
    all_gather x2 -> x0, blocking collectives: 7.2 us -> none  [the longest x1 4.59 us: per_device(): lax.all_gather(owned_lengths, 'mp', axis=0, tiled=True)]
    all_to_all x1 -> x0, starting transfers between devices: 5.38 us -> none  [per_device(): lax.all_to_all(bag_rows, 'dp', split_axis=1, concat_axis=0, tiled=True)]
    unnamed x12 -> x7, local copies, waits for them, and re-layouts: 6.5 us -> 2.03 us
    transpose x0 -> x1, local copies, waits for them, and re-layouts: none -> 2.6 us  [per_device(): grads = pooled_grad.transpose(1, 0, 2).reshape(dp, tables, samples, width)]
  transfers between devices with their start and end apart: 3 -> 0, of which waited for: 1 -> 0; matrix products, arithmetic and copies ran while one was open for 13% -> 0% of each run, Pallas kernels for 0% -> 0%
where the time goes in v1:
time: 109 us
  Pallas kernels  97.1 us (89%)
  other arithmetic  6.45 us (6%)
  local copies, waits for them, and re-layouts  4.63 us (4%)
    pallas_call x1, Pallas kernels, per_device(): pl.pallas_call(functools.partial(exchange_kernel, dp, mp, inner, row_part...  79.5 us
    pallas_call x1, Pallas kernels, per_device(): pl.pallas_call(functools.partial(rows_kernel, slots, 2 if sources % 2 ==...  17.6 us
    transpose x1, local copies, waits for them, and re-layouts, per_device(): grads = pooled_grad.transpose(1, 0, 2).reshape(dp, tables, samples, width)  2.6 us
    sub x1, other arithmetic, per_device(): table_rows - learn_rate * row_grad / jnp.sqrt(new_accum)[..., None]  2.54 us

profile of v1, /device:TPU:11, one launch (start us, length us, event | category | flops | bytes accessed | tf_op | source)
XLA Modules:
  0.0 108.8 jit_solution(6288006134508723304)
XLA Ops:
  0.6 0.0 copy-start.2
  0.6 0.0 copy-start.1
  0.7 1.6 %fusion = s32[128,32,4]{0,2,1:T(4,128)} fusion(s32[128,32,4]{0,2,1:T(4,128)} %param.9, s32[128,32]{0,1:T(8,128)} %param.8), kind=kLoop, calls=%fused_computation.3 | loop fusion | flops 32768 | bytes 147456 | tf_op jit(solution)/shard_map/jit(_where)/select_n | solution.py:265
  2.2 2.6 %copy.10 = bf16[32,128,128]{2,1,0:T(8,128)(2,1)} copy(bf16[32,128,128]{2,0,1:T(8,128)(2,1)} %bitcast.9) | data formatting | bytes 2097152 | tf_op jit(solution)/shard_map/transpose | solution.py:267
  4.8 79.5 %exchange.1 = (bf16[16,2,2,128,128]{4,3,2,1,0:T(8,128)(2,1)}, s32[16,2,8,128]{3,2,1,0:T(8,128)}, f32[1024,1024]{1,0:T(8,128)}) custom-call(bf16[16,2,128,128]{3,2,1,0:T(8,128)(2,1)} %bitcast.7, s32[16,8,128]{2,1,0:T(8,128)} %bitcast.10, bf16[128,1024]{1,0:T(8,128)(2,1)} %din_ref.1, bf16[128,1024]{1,0:T(8,128)(2,1)} %dcot_ref.1), custom_call_target="tpu_custom_call" | custom-call | tf_op jit(solution)/shard_map/exchange/pallas_call | solution.py:272
  84.3 17.6 %rows.1 = f32[2,1024,128]{2,1,0:T(8,128)} custom-call(bf16[32,2,128,128]{3,2,1,0:T(8,128)(2,1)} %bitcast.8, s32[32,8,128]{2,1,0:T(8,128)} %bitcast.11), custom_call_target="tpu_custom_call" | custom-call | tf_op jit(solution)/shard_map/rows/pallas_call | solution.py:298
  101.9 0.0 copy-start
  101.9 1.7 %multiply_reduce_fusion = f32[2,1024]{1,0:T(2,128)S(1)} fusion(f32[2,1024,128]{2,1,0:T(8,128)} %rows.1), kind=kLoop, calls=%fused_computation.1 | loop fusion | flops 522240 | bytes 1056768 | tf_op jit(solution)/shard_map/reduce_sum | solution.py:306
  103.6 0.0 copy-done.2
  103.6 0.6 fusion.1
  104.2 0.0 copy-done.1
  104.2 2.5 %divide_subtract_fusion = f32[2,1024,128]{2,1,0:T(8,128)} fusion(f32[2,1024,128]{2,1,0:T(8,128)S(1)} %copy-done.1, f32[2,1024,128]{2,1,0:T(8,128)} %rows.1, f32[2,1024]{1,0:T(2,128)S(1)} %get-tuple-element.9), kind=kLoop, calls=%fused_computation | loop fusion | flops 786432 | bytes 3153920 | tf_op jit(solution)/shard_map/sub | solution.py:307
  106.8 0.0 copy-done
  106.8 2.0 %copy.12 = f32[1024,1024]{1,0:T(8,128)} copy(f32[1024,1024]{1,0:T(8,128)S(1)} %copy-done) | data formatting | bytes 8388608
Async XLA Ops:
  0.6 103.0 %copy-start.2 = (f32[2,1024]{1,0:T(2,128)S(1)}, f32[2,1024]{1,0:T(2,128)}, u32[]{:S(2)}) copy-start(f32[2,1024]{1,0:T(2,128)} %param.11) | copy-start | bytes 24580
  0.6 103.6 %copy-start.1 = (f32[2,1024,128]{2,1,0:T(8,128)S(1)}, f32[2,1024,128]{2,1,0:T(8,128)}, u32[]{:S(2)}) copy-start(f32[2,1024,128]{2,1,0:T(8,128)} %param.10) | copy-start | bytes 3145732
  101.9 4.9 %copy-start = (f32[1024,1024]{1,0:T(8,128)S(1)}, f32[1024,1024]{1,0:T(8,128)}, u32[]{:S(2)}) copy-start(f32[1024,1024]{1,0:T(8,128)} %get-tuple-element.16) | copy-start | bytes 12582916

commit v2 on v1

--- a/solution.py
+++ b/solution.py
@@ -20,11 +20,11 @@
 
 
 def exchange_kernel(
-    dp, mp, inner, row_parts,
+    dp, mp, inner, row_parts, slots,
     g_ref, i_ref, din_ref, dcot_ref,
-    gbuf, ibuf, dense,
-    abuf, bbuf, part, rbuf,
-    a_send, a_recv, b_send, b_recv, g_send, g_recv, i_send, i_recv,
+    dense, row_grad,
+    gbuf, ibuf, abuf, bbuf, part, rbuf,
+    a_send, a_recv, af_send, af_recv, b_send, b_recv, g_send, g_recv, i_send, i_recv,
     gf_send, gf_recv, if_send, if_recv,
     r_send, r_recv, z_send, z_recv, x_send, x_recv, m_send, m_recv,
 ):
@@ -59,18 +59,20 @@
         return pl.ds(pl.multiple_of((p % col_parts) * cols, 128), cols)
 
     def a_copy(k):
-        p = (mine + 1 + k) % group
-        return remote(din_ref.at[:, row_span(p)], abuf.at[mine], a_send.at[k], a_recv.at[mine], z * inner + p // mp, p % mp)
+        j = (i + 1 + k) % inner
+        return remote(din_ref.at[:, row_span(j * mp)], abuf.at[mine], a_send.at[k], a_recv.at[i], z * inner + j, m)
+
+    def a_pass(k, j, src):
+        return remote(src, abuf.at[j * mp + m], af_send.at[k, j], af_recv.at[m, j], me, (m + 1 + k) % mp)
 
     def b_copy(k):
         p = (mine + 1 + k) % group
         return remote(dcot_ref.at[:, col_span(p)], bbuf.at[mine], b_send.at[k], b_recv.at[mine], z * inner + p // mp, p % mp)
 
-    def start_dense(k):
-        a_copy(k).start()
-        b_copy(k).start()
-
-    loop(group - 1, start_dense)
+    loop(inner - 1, lambda k: a_copy(k).start())
+    loop(group - 1, lambda k: b_copy(k).start())
+    for k in range(mp - 1):
+        a_pass(k, i, din_ref.at[:, row_span(mine)]).start()
 
     def g_copy(k):
         d = (me + 1 + k) % dp
@@ -104,12 +106,29 @@
     abuf[mine] = din_ref[:, row_span(mine)]
     bbuf[mine] = dcot_ref[:, col_span(mine)]
 
-    def wait_dense(k):
+    row_grad[...] = jnp.zeros_like(row_grad)
+
+    def pass_a(k):
+        j = (i + inner - 1 - k) % inner
+        s = j * mp + m
+        remote(abuf.at[s], abuf.at[s], a_send.at[k], a_recv.at[j], me, m).wait_recv()
+        for n in range(mp - 1):
+            a_pass(n, j, abuf.at[s]).start()
+
+    loop(inner - 1, pass_a)
+
+    def wait_a(j):
+        for k in range(mp - 1):
+            q = (m + 1 + k) % mp
+            s = j * mp + q
+            remote(abuf.at[s], abuf.at[s], af_send.at[k, j], af_recv.at[q, j], me, m).wait_recv()
+
+    def wait_b(k):
         s = (mine + 1 + k) % group
-        remote(abuf.at[s], abuf.at[s], a_send.at[k], a_recv.at[s], me, m).wait_recv()
         remote(bbuf.at[s], bbuf.at[s], b_send.at[k], b_recv.at[s], me, m).wait_recv()
 
-    loop(group - 1, wait_dense)
+    loop(group - 1, wait_b)
+    loop(inner, wait_a)
     depth = abuf.shape[0] * abuf.shape[1]
     part[...] = lax.dot_general(
         abuf[...].reshape(depth, rows), bbuf[...].reshape(depth, cols), (((0,), (0,)), ((), ())),
@@ -136,6 +155,40 @@
 
     rbuf[z] = own
 
+    def pass_grads(k):
+        s = (me + dp - 1 - k) % dp
+        remote(gbuf.at[s, m], gbuf.at[s, m], g_send.at[k], g_recv.at[s], me, m).wait_recv()
+        remote(ibuf.at[s, m], ibuf.at[s, m], i_send.at[k], i_recv.at[s], me, m).wait_recv()
+        start_forward(s, gbuf.at[s, m], ibuf.at[s, m])
+
+    loop(dp - 1, pass_grads)
+
+    tables, row_count, width = row_grad.shape
+    samples = i_ref.shape[2]
+    row_iota = lax.broadcasted_iota(jnp.int32, (row_count, samples), 0) + m * row_count
+
+    def add_source(c):
+        s = (me + dp - c) % dp
+        for k in range(mp - 1):
+            q = (m + 1 + k) % mp
+            remote(gbuf.at[s, q], gbuf.at[s, q], gf_send.at[k, s], gf_recv.at[q, s], me, m).wait_recv()
+            remote(ibuf.at[s, q], ibuf.at[s, q], if_send.at[k, s], if_recv.at[q, s], me, m).wait_recv()
+        for t in range(tables):
+            hots = []
+            for u in range(mp):
+                wanted = ibuf[s, u]
+                hot = jnp.zeros((row_count, samples), jnp.float32)
+                for n in range(slots):
+                    one = wanted[t * slots + n : t * slots + n + 1, :]
+                    hot = hot + jnp.where(row_iota == one, 1.0, 0.0)
+                hots.append(hot.astype(jnp.bfloat16))
+            onehot = jnp.concatenate(hots, axis=1)
+            values = gbuf[s, :, t].reshape(mp * samples, width)
+            row_grad[t] += jnp.dot(onehot, values, preferred_element_type=jnp.float32)
+
+    early = dp // 2
+    loop(early, add_source)
+
     def wait_sum(k):
         s = (z + 1 + k) % outer
         remote(rbuf.at[s], rbuf.at[s], r_send.at[k], r_recv.at[s], me, m).wait_recv()
@@ -165,18 +218,12 @@
     loop(outer - 1, lambda k: z_copy(k).start())
     spread(z)
 
-    def pass_grads(k):
-        s = (me + dp - 1 - k) % dp
-        remote(gbuf.at[s, m], gbuf.at[s, m], g_send.at[k], g_recv.at[s], me, m).wait_recv()
-        remote(ibuf.at[s, m], ibuf.at[s, m], i_send.at[k], i_recv.at[s], me, m).wait_recv()
-        start_forward(s, gbuf.at[s, m], ibuf.at[s, m])
-
     def pass_piece(k):
         w = (z + 1 + k) % outer
         remote(at(i, m, w), at(i, m, w), z_send.at[k], z_recv.at[w], me, m).wait_recv()
         spread(w)
 
-    loop(dp - 1, pass_grads)
+    loop(dp - early, lambda c: add_source(early + c))
     loop(outer - 1, pass_piece)
 
     def pass_block(t):
@@ -190,9 +237,6 @@
 
     def end_forward(s):
         for k in range(mp - 1):
-            q = (m + 1 + k) % mp
-            remote(gbuf.at[s, q], gbuf.at[s, q], gf_send.at[k, s], gf_recv.at[q, s], me, m).wait_recv()
-            remote(ibuf.at[s, q], ibuf.at[s, q], if_send.at[k, s], if_recv.at[q, s], me, m).wait_recv()
             for copy in forward(s, k, gbuf.at[s, m], ibuf.at[s, m]):
                 copy.wait_send()
 
@@ -207,15 +251,17 @@
 
     loop(inner * outer, end_block)
 
-    def end_dense(k):
-        a_copy(k).wait_send()
-        b_copy(k).wait_send()
+    def end_a(j):
+        for k in range(mp - 1):
+            a_pass(k, j, abuf.at[j * mp + m]).wait_send()
 
     def end_grads(k):
         g_copy(k).wait_send()
         i_copy(k).wait_send()
 
-    loop(group - 1, end_dense)
+    loop(inner - 1, lambda k: a_copy(k).wait_send())
+    loop(inner, end_a)
+    loop(group - 1, lambda k: b_copy(k).wait_send())
     loop(dp - 1, end_grads)
 
     def end_sum(k):
@@ -224,30 +270,6 @@
 
     loop(outer - 1, end_sum)
     loop((inner - 1) * outer, lambda t: x_copy(t % (inner - 1), t // (inner - 1)).wait_send())
-
-
-def rows_kernel(slots, chunk, g_ref, i_ref, out_ref):
-    tables, row_count = out_ref.shape[0], out_ref.shape[1]
-    samples = i_ref.shape[2]
-    base = lax.axis_index("mp") * row_count
-    row_iota = lax.broadcasted_iota(jnp.int32, (row_count, samples), 0) + base
-    out_ref[...] = jnp.zeros_like(out_ref)
-
-    def add(c):
-        for t in range(tables):
-            hots = []
-            for u in range(chunk):
-                wanted = i_ref[c * chunk + u]
-                hot = jnp.zeros((row_count, samples), jnp.float32)
-                for s in range(slots):
-                    one = wanted[t * slots + s : t * slots + s + 1, :]
-                    hot = hot + jnp.where(row_iota == one, 1.0, 0.0)
-                hots.append(hot.astype(jnp.bfloat16))
-            onehot = jnp.concatenate(hots, axis=1)
-            values = g_ref[pl.ds(c * chunk, chunk), t].reshape(chunk * samples, g_ref.shape[3])
-            out_ref[t] += jnp.dot(onehot, values, preferred_element_type=jnp.float32)
-
-    loop(i_ref.shape[0] // chunk, add)
 
 
 def per_device(dp, mp, pooled_grad, bag_lengths, bag_rows, table_rows, row_accum, dense_input, dense_cotangent):
@@ -257,7 +279,7 @@
     inner = 4 if dp % 4 == 0 else 1
     outer = dp // inner
     group = inner * mp
-    row_parts = 2 if group % 2 == 0 else 1
+    row_parts = 2 if inner % 2 == 0 else 1
     in_width, out_width = dense_input.shape[1], dense_cotangent.shape[1]
     rows, cols = in_width // row_parts, out_width // (group // row_parts)
 
@@ -269,21 +291,22 @@
     vmem = pl.BlockSpec(memory_space=pltpu.VMEM)
     dma = pltpu.SemaphoreType.DMA
     pairs = max(1, mp - 1)
-    gathered, targets, dense_grad = pl.pallas_call(
-        functools.partial(exchange_kernel, dp, mp, inner, row_parts),
+    dense_grad, row_grad = pl.pallas_call(
+        functools.partial(exchange_kernel, dp, mp, inner, row_parts, slots),
         out_shape=(
-            jax.ShapeDtypeStruct((dp, mp, tables, samples, width), jnp.bfloat16),
-            jax.ShapeDtypeStruct((dp, mp, tables * slots, samples), jnp.int32),
             jax.ShapeDtypeStruct((in_width, out_width), jnp.float32),
+            jax.ShapeDtypeStruct((tables, row_count, width), jnp.float32),
         ),
         in_specs=[vmem] * 4,
-        out_specs=(vmem,) * 3,
+        out_specs=(vmem,) * 2,
         scratch_shapes=[
+            pltpu.VMEM((dp, mp, tables, samples, width), jnp.bfloat16),
+            pltpu.VMEM((dp, mp, tables * slots, samples), jnp.int32),
             pltpu.VMEM((group, samples, rows), jnp.bfloat16),
             pltpu.VMEM((group, samples, cols), jnp.bfloat16),
             pltpu.VMEM((rows, cols), jnp.float32),
             pltpu.VMEM((outer, rows // outer, cols), jnp.float32),
-            dma((group,)), dma((group,)), dma((group,)), dma((group,)),
+            dma((inner,)), dma((inner,)), dma((pairs, inner)), dma((mp, inner)), dma((group,)), dma((group,)),
             dma((dp,)), dma((dp,)), dma((dp,)), dma((dp,)),
             dma((pairs, dp)), dma((mp, dp)), dma((pairs, dp)), dma((mp, dp)),
             dma((outer,)), dma((outer,)), dma((outer,)), dma((outer,)),
@@ -293,15 +316,6 @@
         compiler_params=pltpu.CompilerParams(collective_id=0, has_side_effects=True),
         name="exchange",
     )(grads, target, dense_input, dense_cotangent)
-
-    sources = dp * mp
-    row_grad = pl.pallas_call(
-        functools.partial(rows_kernel, slots, 2 if sources % 2 == 0 else 1),
-        out_shape=jax.ShapeDtypeStruct((tables, row_count, width), jnp.float32),
-        in_specs=[vmem] * 2,
-        out_specs=vmem,
-        name="rows",
-    )(gathered.reshape(sources, tables, samples, width), targets.reshape(sources, tables * slots, samples))
 
     new_accum = row_accum + jnp.mean(row_grad * row_grad, axis=-1)
     new_rows = table_rows - learn_rate * row_grad / jnp.sqrt(new_accum)[..., None]

time: 109 us -> 91.3 us (0.84)
  Pallas kernels: 97.1 us -> 79.3 us
    pallas_call x1 -> x0, Pallas kernels: 17.6 us -> none  [per_device(): pl.pallas_call(functools.partial(rows_kernel, slots, 2 if sources % 2 ==...]
where the time goes in v2:
time: 91.3 us; the launch traced here: 91.1 us
  Pallas kernels  79.3 us (87%)
  other arithmetic  6.45 us (7%)
  local copies, waits for them, and re-layouts  4.63 us (5%)
    pallas_call x1, Pallas kernels, per_device(): pl.pallas_call(functools.partial(exchange_kernel, dp, mp, inner, row_part...  79.3 us
    transpose x1, local copies, waits for them, and re-layouts, per_device(): grads = pooled_grad.transpose(1, 0, 2).reshape(dp, tables, samples, width)  2.6 us
    sub x1, other arithmetic, per_device(): table_rows - learn_rate * row_grad / jnp.sqrt(new_accum)[..., None]  2.54 us
    unnamed x7, local copies, waits for them, and re-layouts  2.03 us

profile of v2, /device:TPU:11, one launch (start us, length us, event | category | flops | bytes accessed | tf_op | source)
XLA Modules:
  0.0 91.1 jit_solution(16351927307491241613)
XLA Ops:
  0.6 0.0 copy-start.2
  0.6 0.0 copy-start.1
  0.7 1.6 %fusion = s32[128,32,4]{0,2,1:T(4,128)} fusion(s32[128,32,4]{0,2,1:T(4,128)} %param.9, s32[128,32]{0,1:T(8,128)} %param.8), kind=kLoop, calls=%fused_computation.3 | loop fusion | flops 32768 | bytes 147456 | tf_op jit(solution)/shard_map/jit(_where)/select_n | solution.py:287
  2.2 2.6 %copy.10 = bf16[32,128,128]{2,1,0:T(8,128)(2,1)} copy(bf16[32,128,128]{2,0,1:T(8,128)(2,1)} %bitcast.6) | data formatting | bytes 2097152 | tf_op jit(solution)/shard_map/transpose | solution.py:289
  4.8 79.3 %exchange.1 = (f32[1024,1024]{1,0:T(8,128)}, f32[2,1024,128]{2,1,0:T(8,128)}) custom-call(bf16[16,2,128,128]{3,2,1,0:T(8,128)(2,1)} %bitcast.5, s32[16,8,128]{2,1,0:T(8,128)} %bitcast.7, bf16[128,1024]{1,0:T(8,128)(2,1)} %din_ref.1, bf16[128,1024]{1,0:T(8,128)(2,1)} %dcot_ref.1), custom_call_target="tpu_custom_call" | custom-call | tf_op jit(solution)/shard_map/exchange/pallas_call | solution.py:294
  84.2 0.0 copy-start
  84.2 1.7 %multiply_reduce_fusion = f32[2,1024]{1,0:T(2,128)S(1)} fusion(f32[2,1024,128]{2,1,0:T(8,128)} %get-tuple-element.5), kind=kLoop, calls=%fused_computation.1 | loop fusion | flops 522240 | bytes 1056768 | tf_op jit(solution)/shard_map/reduce_sum | solution.py:320
  85.9 0.0 copy-done.2
  85.9 0.6 fusion.1
  86.5 0.0 copy-done.1
  86.6 2.5 %divide_subtract_fusion = f32[2,1024,128]{2,1,0:T(8,128)} fusion(f32[2,1024,128]{2,1,0:T(8,128)S(1)} %copy-done.1, f32[2,1024,128]{2,1,0:T(8,128)} %get-tuple-element.5, f32[2,1024]{1,0:T(2,128)S(1)} %get-tuple-element.7), kind=kLoop, calls=%fused_computation | loop fusion | flops 786432 | bytes 3153920 | tf_op jit(solution)/shard_map/sub | solution.py:321
  89.1 0.0 copy-done
  89.1 2.0 %copy.12 = f32[1024,1024]{1,0:T(8,128)} copy(f32[1024,1024]{1,0:T(8,128)S(1)} %copy-done) | data formatting | bytes 8388608
Async XLA Ops:
  0.6 85.3 %copy-start.2 = (f32[2,1024]{1,0:T(2,128)S(1)}, f32[2,1024]{1,0:T(2,128)}, u32[]{:S(2)}) copy-start(f32[2,1024]{1,0:T(2,128)} %param.11) | copy-start | bytes 24580
  0.6 85.9 %copy-start.1 = (f32[2,1024,128]{2,1,0:T(8,128)S(1)}, f32[2,1024,128]{2,1,0:T(8,128)}, u32[]{:S(2)}) copy-start(f32[2,1024,128]{2,1,0:T(8,128)} %param.10) | copy-start | bytes 3145732
  84.2 4.9 %copy-start = (f32[1024,1024]{1,0:T(8,128)S(1)}, f32[1024,1024]{1,0:T(8,128)}, u32[]{:S(2)}) copy-start(f32[1024,1024]{1,0:T(8,128)} %get-tuple-element.14) | copy-start | bytes 12582916

commit v3 on v2

--- a/solution.py
+++ b/solution.py
@@ -26,7 +26,7 @@
     gbuf, ibuf, abuf, bbuf, part, rbuf,
     a_send, a_recv, af_send, af_recv, b_send, b_recv, g_send, g_recv, i_send, i_recv,
     gf_send, gf_recv, if_send, if_recv,
-    r_send, r_recv, z_send, z_recv, x_send, x_recv, m_send, m_recv,
+    r_send, r_recv, z_send, z_recv, x_send, x_recv, y_send, y_recv, m_send, m_recv,
 ):
     me = lax.axis_index("dp")
     m = lax.axis_index("mp")
@@ -203,15 +203,29 @@
         w = (z + 1 + k) % outer
         return remote(at(i, m, z), at(i, m, z), z_send.at[k], z_recv.at[z], w * inner + i, m)
 
+    sides = (i + 1 - 2 * (i % 2), (i + 2) % inner)
+    across = sides[0] + sides[1] - i
+    half = piece // 2
+
     def x_copy(k, w):
-        j = (i + 1 + k) % inner
-        return remote(at(i, m, w), at(i, m, w), x_send.at[k, w], x_recv.at[i, w], z * inner + j, m)
+        return remote(at(i, m, w), at(i, m, w), x_send.at[k, w], x_recv.at[k, w], z * inner + sides[k], m)
+
+    def half_at(j, k, w):
+        p = j * mp + m
+        top = pl.multiple_of((p // col_parts) * rows + w * piece + k * half, 8)
+        return dense.at[pl.ds(top, half), col_span(p)]
+
+    def y_copy(k, w):
+        here = half_at(sides[k], k, w)
+        return remote(here, here, y_send.at[k, w], y_recv.at[k, w], z * inner + sides[1 - k], m)
 
     def m_copy(k, j, w):
         return remote(at(j, m, w), at(j, m, w), m_send.at[k, j, w], m_recv.at[m, j, w], me, (m + 1 + k) % mp)
 
     def spread(w):
-        loop(inner - 1, lambda k: x_copy(k, w).start())
+        if inner > 1:
+            for k in range(2):
+                x_copy(k, w).start()
         for k in range(mp - 1):
             m_copy(k, i, w).start()
 
@@ -223,17 +237,36 @@
         remote(at(i, m, w), at(i, m, w), z_send.at[k], z_recv.at[w], me, m).wait_recv()
         spread(w)
 
-    loop(dp - early, lambda c: add_source(early + c))
-    loop(outer - 1, pass_piece)
-
-    def pass_block(t):
-        k, w = t % (inner - 1), (z + t // (inner - 1)) % outer
-        j = (i + 1 + k) % inner
-        remote(at(j, m, w), at(j, m, w), x_send.at[k, w], x_recv.at[j, w], me, m).wait_recv()
+    per = (dp - early) // outer
+
+    def late(k):
+        loop(per, lambda c: add_source(early + k * per + c))
+        pass_piece(k)
+
+    loop(outer - 1, late)
+    done = early + (outer - 1) * per
+    loop(dp - done, lambda c: add_source(done + c))
+
+    def pass_side(t):
+        w = (z + t) % outer
+        for k in range(2):
+            j = sides[k]
+            remote(at(j, m, w), at(j, m, w), x_send.at[k, w], x_recv.at[k, w], me, m).wait_recv()
+            y_copy(k, w).start()
+            for n in range(mp - 1):
+                m_copy(n, j, w).start()
+
+    def pass_across(t):
+        w = (z + t) % outer
+        for k in range(2):
+            here = half_at(across, k, w)
+            remote(here, here, y_send.at[k, w], y_recv.at[k, w], me, m).wait_recv()
         for n in range(mp - 1):
-            m_copy(n, j, w).start()
-
-    loop((inner - 1) * outer, pass_block)
+            m_copy(n, across, w).start()
+
+    if inner > 1:
+        loop(outer, pass_side)
+        loop(outer, pass_across)
 
     def end_forward(s):
         for k in range(mp - 1):
@@ -269,7 +302,14 @@
         z_copy(k).wait_send()
 
     loop(outer - 1, end_sum)
-    loop((inner - 1) * outer, lambda t: x_copy(t % (inner - 1), t // (inner - 1)).wait_send())
+
+    def end_side(w):
+        for k in range(2):
+            x_copy(k, w).wait_send()
+            y_copy(k, w).wait_send()
+
+    if inner > 1:
+        loop(outer, end_side)
 
 
 def per_device(dp, mp, pooled_grad, bag_lengths, bag_rows, table_rows, row_accum, dense_input, dense_cotangent):
@@ -310,7 +350,7 @@
             dma((dp,)), dma((dp,)), dma((dp,)), dma((dp,)),
             dma((pairs, dp)), dma((mp, dp)), dma((pairs, dp)), dma((mp, dp)),
             dma((outer,)), dma((outer,)), dma((outer,)), dma((outer,)),
-            dma((inner, outer)), dma((inner, outer)),
+            dma((2, outer)), dma((2, outer)), dma((2, outer)), dma((2, outer)),
             dma((pairs, inner, outer)), dma((mp, inner, outer)),
         ],
         compiler_params=pltpu.CompilerParams(collective_id=0, has_side_effects=True),

time: 91.3 us -> 87.8 us (0.962); the launches traced: 91.1 us -> 86.6 us
  Pallas kernels: 79.3 us -> 74.8 us
    pallas_call x1, Pallas kernels: 79.3 us -> 74.8 us  [per_device(): pl.pallas_call(functools.partial(exchange_kernel, dp, mp, inner, row_part...]
where the time goes in v3:
time: 87.8 us; the launch traced here: 86.6 us
  Pallas kernels  74.8 us (85%)
  other arithmetic  6.45 us (7%)
  local copies, waits for them, and re-layouts  4.63 us (5%)
    pallas_call x1, Pallas kernels, per_device(): pl.pallas_call(functools.partial(exchange_kernel, dp, mp, inner, row_part...  74.8 us
    transpose x1, local copies, waits for them, and re-layouts, per_device(): grads = pooled_grad.transpose(1, 0, 2).reshape(dp, tables, samples, width)  2.6 us
    sub x1, other arithmetic, per_device(): table_rows - learn_rate * row_grad / jnp.sqrt(new_accum)[..., None]  2.54 us
    unnamed x7, local copies, waits for them, and re-layouts  2.03 us

profile of v3, /device:TPU:11, one launch (start us, length us, event | category | flops | bytes accessed | tf_op | source)
XLA Modules:
  0.0 86.6 jit_solution(16722482692692978484)
XLA Ops:
  0.6 0.0 copy-start.2
  0.6 0.0 copy-start.1
  0.7 1.6 %fusion = s32[128,32,4]{0,2,1:T(4,128)} fusion(s32[128,32,4]{0,2,1:T(4,128)} %param.9, s32[128,32]{0,1:T(8,128)} %param.8), kind=kLoop, calls=%fused_computation.3 | loop fusion | flops 32768 | bytes 147456 | tf_op jit(solution)/shard_map/jit(_where)/select_n | solution.py:327
  2.2 2.6 %copy.10 = bf16[32,128,128]{2,1,0:T(8,128)(2,1)} copy(bf16[32,128,128]{2,0,1:T(8,128)(2,1)} %bitcast.6) | data formatting | bytes 2097152 | tf_op jit(solution)/shard_map/transpose | solution.py:329
  4.8 74.8 %exchange.1 = (f32[1024,1024]{1,0:T(8,128)}, f32[2,1024,128]{2,1,0:T(8,128)}) custom-call(bf16[16,2,128,128]{3,2,1,0:T(8,128)(2,1)} %bitcast.5, s32[16,8,128]{2,1,0:T(8,128)} %bitcast.7, bf16[128,1024]{1,0:T(8,128)(2,1)} %din_ref.1, bf16[128,1024]{1,0:T(8,128)(2,1)} %dcot_ref.1), custom_call_target="tpu_custom_call" | custom-call | tf_op jit(solution)/shard_map/exchange/pallas_call | solution.py:334
  79.6 0.0 copy-start
  79.6 1.7 %multiply_reduce_fusion = f32[2,1024]{1,0:T(2,128)S(1)} fusion(f32[2,1024,128]{2,1,0:T(8,128)} %get-tuple-element.5), kind=kLoop, calls=%fused_computation.1 | loop fusion | flops 522240 | bytes 1056768 | tf_op jit(solution)/shard_map/reduce_sum | solution.py:360
  81.4 0.0 copy-done.2
  81.4 0.6 fusion.1
  82.0 0.0 copy-done.1
  82.0 2.5 %divide_subtract_fusion = f32[2,1024,128]{2,1,0:T(8,128)} fusion(f32[2,1024,128]{2,1,0:T(8,128)S(1)} %copy-done.1, f32[2,1024,128]{2,1,0:T(8,128)} %get-tuple-element.5, f32[2,1024]{1,0:T(2,128)S(1)} %get-tuple-element.7), kind=kLoop, calls=%fused_computation | loop fusion | flops 786432 | bytes 3153920 | tf_op jit(solution)/shard_map/sub | solution.py:361
  84.5 0.0 copy-done
  84.5 2.0 %copy.12 = f32[1024,1024]{1,0:T(8,128)} copy(f32[1024,1024]{1,0:T(8,128)S(1)} %copy-done) | data formatting | bytes 8388608
Async XLA Ops:
  0.6 80.7 %copy-start.2 = (f32[2,1024]{1,0:T(2,128)S(1)}, f32[2,1024]{1,0:T(2,128)}, u32[]{:S(2)}) copy-start(f32[2,1024]{1,0:T(2,128)} %param.11) | copy-start | bytes 24580
  0.6 81.4 %copy-start.1 = (f32[2,1024,128]{2,1,0:T(8,128)S(1)}, f32[2,1024,128]{2,1,0:T(8,128)}, u32[]{:S(2)}) copy-start(f32[2,1024,128]{2,1,0:T(8,128)} %param.10) | copy-start | bytes 3145732
  79.6 4.9 %copy-start = (f32[1024,1024]{1,0:T(8,128)S(1)}, f32[1024,1024]{1,0:T(8,128)}, u32[]{:S(2)}) copy-start(f32[1024,1024]{1,0:T(8,128)} %get-tuple-element.14) | copy-start | bytes 12582916
